TPU v7x, 32 devices: a whole 2x2x4 slice. The times are simulated.
32 devices in a mesh: rows: 4 (over y, x), feat: 8 (over z, core).
Axes of the slice: x: 2, y: 2, z: 4, core: 2. Of those that a mesh axis runs over, the one named last changes fastest.
Arguments:
- bins: int32 [256, 32768], P(None, ('rows', 'feat')), may hold values from 0 to 255
- leaf: int32 [32768], P(('rows', 'feat')), may hold values from 0 to 1
- grad: bfloat16 [32, 32768], P(None, ('rows', 'feat')), may hold values from -15.55 to 15.55
- hess: bfloat16 [32, 32768], P(None, ('rows', 'feat')), may hold values from 0.049804688 to 1
Outputs:
- gains: float32 [256, 2, 256], P(('rows', 'feat'))
- best: float32 [2], replicated
All inputs are finite; a program needn't handle non-finite values.
Results may differ from a plain program's by a relative error of at most 0.0003.
Values may be sent and summed in bfloat16 or wider, within the bound.
A program may use at most 128 MiB of HBM per device.

v0:
```python
import math
import jax
import jax.numpy as jnp
from jax import lax
from jax.sharding import PartitionSpec as P

F = 256
B = 256
LEAVES = 2


def leaf_weighted(both, leaf_row, leaves):
    nodes = jnp.arange(leaves, dtype=jnp.float32)[:, None]
    hot = (leaf_row.astype(jnp.float32) == nodes).astype(jnp.bfloat16)
    return (hot[:, None, :] * both[None, :, :]).reshape(leaves * both.shape[0], both.shape[1])


def bin_counts(codes, weighted, bin_total):
    levels = jnp.arange(bin_total, dtype=jnp.int32)
    onehot = (codes[:, :, None] == levels).astype(jnp.bfloat16)
    return jnp.einsum("frb,cr->fbc", onehot, weighted, preferred_element_type=jnp.float32)


def split_gains(hist, totals, outputs):
    count = hist.shape[0]
    cum = jnp.cumsum(hist, axis=1).reshape(count, B, LEAVES, 2, outputs)
    tot = totals.reshape(LEAVES, 2, outputs)
    left_grad = cum[:, :, :, 0, :]
    left_hess = cum[:, :, :, 1, :]
    all_grad = tot[:, 0, :]
    all_hess = tot[:, 1, :]
    right_grad = all_grad - left_grad
    right_hess = all_hess - left_hess
    score = (
        left_grad * left_grad / (left_hess + 1.0)
        + right_grad * right_grad / (right_hess + 1.0)
        - all_grad * all_grad / (all_hess + 1.0)
    )
    gains = 0.5 / outputs * jnp.sum(score, axis=-1)
    return jnp.transpose(gains, (0, 2, 1))


def shards(bins, leaf, grad, hess):
    outputs = grad.shape[0]
    shard = bins.shape[1]
    devices = lax.axis_size("rows") * lax.axis_size("feat")
    owned = F // devices
    both = jnp.concatenate([grad, hess], axis=0)
    leaf_row = leaf[None, :]
    weighted = leaf_weighted(both, leaf_row, LEAVES)
    columns = weighted.shape[0]
    codes_mine = lax.all_to_all(bins, ("rows", "feat"), split_axis=0, concat_axis=1, tiled=True)
    initial = jnp.zeros((owned, B, columns), jnp.float32)
    both_piece = lax.all_gather(both, ("rows", "feat"), axis=1, tiled=True)
    leaf_piece = lax.all_gather(leaf_row.astype(jnp.bfloat16), ("rows", "feat"), axis=1, tiled=True)
    length = both_piece.shape[1]
    width = math.gcd(length, 8 * shard)

    def step(index, total):
        offset = index * width
        part_codes = lax.dynamic_slice_in_dim(codes_mine, offset, width, 1)
        part_both = lax.dynamic_slice_in_dim(both_piece, offset, width, 1)
        part_leaf = lax.dynamic_slice_in_dim(leaf_piece, offset, width, 1)
        return total + bin_counts(part_codes, leaf_weighted(part_both, part_leaf, LEAVES), B)

    hist = lax.fori_loop(0, length // width, step, initial)
    totals = lax.psum(jnp.sum(weighted, axis=1, dtype=jnp.float32), ("rows", "feat"))
    gains = split_gains(hist, totals, outputs)
    best = lax.pmax(jnp.max(gains, axis=(0, 2)), ("rows", "feat"))
    return (gains, best)


def solution(mesh):
    return jax.shard_map(
        shards,
        mesh=mesh,
        in_specs=(
            P(None, ("rows", "feat")),
            P(("rows", "feat")),
            P(None, ("rows", "feat")),
            P(None, ("rows", "feat")),
        ),
        out_specs=(P(("rows", "feat"), None, None), P()),
        check_vma=False,
    )
```

profile of v0, /device:TPU:0, one launch (start us, length us, event | category | flops | bytes accessed | tf_op | source)
XLA Modules:
  0.0 226.1 jit_solution(3870619815995787336)
XLA Ops:
  7.2 0.0 copy-start.2
  7.2 0.0 all-gather.3.cloned.1.call-start
  7.2 0.8 constant_dynamic-update-slice_fusion.1
  8.1 0.8 constant_dynamic-update-slice_fusion
  8.9 0.0 copy-start
  8.9 0.6 copy-done
  9.5 0.0 all-gather.3.cloned.1.call-update
  9.6 0.0 copy-start.1
  9.6 7.3 %all-to-all-start = ((s32[32,8,1024]{2,1,0:T(8,128)}), s32[32,8,1024]{2,1,0:T(8,128)S(1)}, u32[]{:S(2)}, u32[]{:S(2)}) async-start(s32[32,8,1024]{2,1,0:T(8,128)} %bitcast.44), calls=%async_computation | async-start | bytes 2097152 | tf_op jit(solution)/shard_map/all_to_all | solution.py:52
  16.9 0.0 copy-done.2
  17.0 0.0 copy-done.1
  17.0 0.1 convert_reduce_fusion
  17.1 0.1 reshape.98
  17.2 60.4 %all-gather = bf16[32768]{0:T(1024)(128)(2,1)S(1)} all-gather(bf16[1024]{0:T(1024)(128)(2,1)S(1)} %get-tuple-element.128), channel_id=2, replica_groups=mesh['rows'=4,'feat'=8] {'rows','feat'}, dimensions={0}, use_global_device_ids=true | all-gather | bytes 67584 | tf_op jit(solution)/shard_map/all_gather | solution.py:55
  77.6 0.1 reshape.101
  77.6 37.5 %psum.7 = f32[2,2,32]{2,1,0:T(2,128)S(1)} all-reduce(f32[2,2,32]{2,1,0:T(2,128)S(1)} %reshape.98), channel_id=1, replica_groups=mesh['rows'=4,'feat'=8] {'rows','feat'}, use_global_device_ids=true, to_apply=%region_5.6 | all-reduce | flops 128 | bytes 1024 | tf_op jit(solution)/shard_map/psum | solution.py:67
  115.2 0.0 all-to-all-done
  115.2 0.0 all-gather.3.cloned.1.call-done
  115.2 58.8 %while.14 = (s32[]{:T(128)}, f32[8,256,128]{2,1,0:T(8,128)}, s32[8,32768]{1,0:T(8,128)S(1)}, bf16[1,32768]{1,0:T(2,128)(2,1)S(1)}, bf16[64,32768]{1,0:T(8,128)(2...) while((s32[]{:T(128)}, f32[8,256,128]{2,1,0:T(8,128)}, s32[8,32768]{1,0:T(8,128)S(1)}, ...), condition=%wide.region_1.0_spmd.clone, body=%wide.region_0.0_spmd.clone.sunk | while | flops 4313358336 | bytes 10371233 | solution.py:66
  115.2 1.3 constant_dynamic-slice_fusion.4
  116.6 0.2 broadcast_multiply_fusion.2
  116.8 12.3 %fusion.12 = f32[8,256,128]{2,1,0:T(8,128)} fusion(bf16[128,8192,1]{1,0,2:T(8,128)(2,1)S(1)} %bitcast.39, s32[8,8192]{1,0:T(8,128)S(1)} %constant_dynamic-slice_fusion.5, f32[8,256,128]{2,1,0:T(8,128)} %get-tuple-element.172, pred[]{:T(512)S(6)} %compare.3), kind=kOutput, calls=%fused_computation.3.clone.1 | convolution fusion | flops 4312268800 | bytes 4456449 | tf_op jit(solution)/shard_map/while/body/eval_jaxpr/frb,cr->fbc/dot_general | solution.py:21
  129.2 1.3 constant_dynamic-slice_fusion.4
  130.6 0.2 broadcast_multiply_fusion.2
  130.8 13.3 %fusion.12 = f32[8,256,128]{2,1,0:T(8,128)} fusion(bf16[128,8192,1]{1,0,2:T(8,128)(2,1)S(1)} %bitcast.39, s32[8,8192]{1,0:T(8,128)S(1)} %constant_dynamic-slice_fusion.5, f32[8,256,128]{2,1,0:T(8,128)} %get-tuple-element.172, pred[]{:T(512)S(6)} %compare.3), kind=kOutput, calls=%fused_computation.3.clone.1 | convolution fusion | flops 4312268800 | bytes 4456449 | tf_op jit(solution)/shard_map/while/body/eval_jaxpr/frb,cr->fbc/dot_general | solution.py:21
  144.1 1.3 constant_dynamic-slice_fusion.4
  145.5 0.2 broadcast_multiply_fusion.2
  145.7 13.4 %fusion.12 = f32[8,256,128]{2,1,0:T(8,128)} fusion(bf16[128,8192,1]{1,0,2:T(8,128)(2,1)S(1)} %bitcast.39, s32[8,8192]{1,0:T(8,128)S(1)} %constant_dynamic-slice_fusion.5, f32[8,256,128]{2,1,0:T(8,128)} %get-tuple-element.172, pred[]{:T(512)S(6)} %compare.3), kind=kOutput, calls=%fused_computation.3.clone.1 | convolution fusion | flops 4312268800 | bytes 4456449 | tf_op jit(solution)/shard_map/while/body/eval_jaxpr/frb,cr->fbc/dot_general | solution.py:21
  159.1 1.3 constant_dynamic-slice_fusion.4
  160.4 0.2 broadcast_multiply_fusion.2
  160.6 13.4 %fusion.12 = f32[8,256,128]{2,1,0:T(8,128)} fusion(bf16[128,8192,1]{1,0,2:T(8,128)(2,1)S(1)} %bitcast.39, s32[8,8192]{1,0:T(8,128)S(1)} %constant_dynamic-slice_fusion.5, f32[8,256,128]{2,1,0:T(8,128)} %get-tuple-element.172, pred[]{:T(512)S(6)} %compare.3), kind=kOutput, calls=%fused_computation.3.clone.1 | convolution fusion | flops 4312268800 | bytes 4456449 | tf_op jit(solution)/shard_map/while/body/eval_jaxpr/frb,cr->fbc/dot_general | solution.py:21
  174.0 1.8 fusion.3
  175.8 0.1 fusion.5
  175.9 0.1 broadcast_add_fusion
  176.0 0.4 copy.15
  176.4 0.4 subtract_reduce_fusion
  176.8 0.7 multiply_reduce_fusion
  177.5 41.8 %pmax.7 = f32[2]{0:T(128)} all-reduce(f32[2]{0:T(128)S(1)} %get-tuple-element.125), channel_id=1, replica_groups=mesh['rows'=4,'feat'=8] {'rows','feat'}, use_global_device_ids=true, to_apply=%region_8.9 | all-reduce | flops 2 | bytes 16 | tf_op jit(solution)/shard_map/pmax | solution.py:69
  (18 shorter events, 0.4 us)
Async XLA Ops:
  7.2 9.8 %copy-start.2 = (s32[1024]{0:T(1024)S(1)}, s32[1024]{0:T(1024)}, u32[]{:S(2)}) copy-start(s32[1024]{0:T(1024)} %param.7) | copy-start | bytes 12292
  7.2 108.0 %all-gather.3.cloned.1.call-start = ((), (), s32[]{:S(2)}) async-start(), calls=%async_computation.1 | async-start | bytes 4325376 | tf_op jit(solution)/shard_map/all_gather | solution.py:54
  8.9 0.6 copy-start
  9.6 7.4 %copy-start.1 = (bf16[64,1024]{1,0:T(8,128)(2,1)S(1)}, bf16[64,1024]{1,0:T(8,128)(2,1)}, u32[]{:S(2)}) copy-start(bf16[64,1024]{1,0:T(8,128)(2,1)} %copy-done) | copy-start | bytes 393220
  9.6 105.6 %all-to-all-start = ((s32[32,8,1024]{2,1,0:T(8,128)}), s32[32,8,1024]{2,1,0:T(8,128)S(1)}, u32[]{:S(2)}, u32[]{:S(2)}) async-start(s32[32,8,1024]{2,1,0:T(8,128)} %bitcast.44), calls=%async_computation | async-start | bytes 2097152 | tf_op jit(solution)/shard_map/all_to_all | solution.py:52
Sparse Core Ops, SparseCore 0:
  11.0 66.5 all-gather.2
where the time goes:
time: 227 us; the launch traced here: 226 us
  blocking collectives  140 us (62%)
  matrix products  52.4 us (23%)
  between operations  14.1 us (6%)
  local copies, waits for them, and re-layouts  8.17 us (4%)
  starting transfers between devices  7.37 us (3%)
  other arithmetic  4.15 us (2%)
    all_gather x1, blocking collectives, shards(): lax.all_gather(leaf_row.astype(jnp.bfloat16), ('rows', 'feat'), axis=1, t...  60.4 us
    dot_general x4, matrix products, bin_counts(): jnp.einsum('frb,cr->fbc', onehot, weighted, preferred_element_type=jnp.fl...  52.4 us
    pmax x1, blocking collectives, shards(): best = lax.pmax(jnp.max(gains, axis=(0, 2)), ('rows', 'feat'))  41.8 us
    psum x1, blocking collectives, shards(): lax.psum(jnp.sum(weighted, axis=1, dtype=jnp.float32), ('rows', 'feat'))  37.5 us
    all_to_all x1, starting transfers between devices, shards(): lax.all_to_all(bins, ('rows', 'feat'), split_axis=0, concat_axis=1, tiled...  7.33 us
    dynamic_slice x4, local copies, waits for them, and re-layouts, step(): part_both = lax.dynamic_slice_in_dim(both_piece, offset, width, 1)  5.17 us
  transfers between devices with their start and end apart: 2, of which 0 were waited for; matrix products, arithmetic and copies ran while one was open for 0% of the time, Pallas kernels for 0%

commit v1 on v0

--- a/solution.py
+++ b/solution.py
@@ -64,7 +64,7 @@
         return total + bin_counts(part_codes, leaf_weighted(part_both, part_leaf, LEAVES), B)
 
     hist = lax.fori_loop(0, length // width, step, initial)
-    totals = lax.psum(jnp.sum(weighted, axis=1, dtype=jnp.float32), ("rows", "feat"))
+    totals = lax.psum(lax.psum(jnp.sum(weighted, axis=1, dtype=jnp.float32), "rows"), "feat")
     gains = split_gains(hist, totals, outputs)
     best = lax.pmax(jnp.max(gains, axis=(0, 2)), ("rows", "feat"))
     return (gains, best)

time: 227 us -> 199 us (0.88)
  blocking collectives: 140 us -> 111 us
    psum x1 -> x2, blocking collectives: 37.5 us -> 24.4 us  [the longest x1 13.9 us: shards(): lax.psum(lax.psum(jnp.sum(weighted, axis=1, dtype=jnp.float32), 'rows'),...]
    all_gather x1, blocking collectives: 60.4 us -> 49.6 us  [shards(): lax.all_gather(leaf_row.astype(jnp.bfloat16), ('rows', 'feat'), axis=1, t...]
    pmax x1, blocking collectives: 41.8 us -> 36.8 us  [shards(): best = lax.pmax(jnp.max(gains, axis=(0, 2)), ('rows', 'feat'))]
where the time goes in v1:
time: 199 us; the launch traced here: 197 us
  blocking collectives  111 us (56%)
  matrix products  52.4 us (26%)
  between operations  14.1 us (7%)
  local copies, waits for them, and re-layouts  8.26 us (4%)
  starting transfers between devices  7.37 us (4%)
  other arithmetic  4.15 us (2%)
    dot_general x4, matrix products, bin_counts(): jnp.einsum('frb,cr->fbc', onehot, weighted, preferred_element_type=jnp.fl...  52.4 us
    all_gather x1, blocking collectives, shards(): lax.all_gather(leaf_row.astype(jnp.bfloat16), ('rows', 'feat'), axis=1, t...  49.6 us
    pmax x1, blocking collectives, shards(): best = lax.pmax(jnp.max(gains, axis=(0, 2)), ('rows', 'feat'))  36.8 us
    psum x1, blocking collectives, shards(): lax.psum(lax.psum(jnp.sum(weighted, axis=1, dtype=jnp.float32), 'rows'),...  13.9 us
    psum x1, blocking collectives, shards(): lax.psum(jnp.sum(weighted, axis=1, dtype=jnp.float32), 'rows')  10.5 us
    all_to_all x1, starting transfers between devices, shards(): lax.all_to_all(bins, ('rows', 'feat'), split_axis=0, concat_axis=1, tiled...  7.33 us
    dynamic_slice x4, local copies, waits for them, and re-layouts, step(): part_both = lax.dynamic_slice_in_dim(both_piece, offset, width, 1)  5.17 us
  transfers between devices with their start and end apart: 2, of which 0 were waited for; matrix products, arithmetic and copies ran while one was open for 0% of the time, Pallas kernels for 0%

profile of v1, /device:TPU:0, one launch (start us, length us, event | category | flops | bytes accessed | tf_op | source)
XLA Modules:
  0.0 197.4 jit_solution(46450709776280863)
XLA Ops:
  7.2 0.0 copy-start.2
  7.2 0.0 all-gather.3.cloned.1.call-start
  7.2 0.8 constant_dynamic-update-slice_fusion.1
  8.1 0.8 constant_dynamic-update-slice_fusion
  8.9 0.0 copy-start
  8.9 0.6 copy-done
  9.5 0.0 all-gather.3.cloned.1.call-update
  9.6 0.0 copy-start.1
  9.6 7.3 %all-to-all-start = ((s32[32,8,1024]{2,1,0:T(8,128)}), s32[32,8,1024]{2,1,0:T(8,128)S(1)}, u32[]{:S(2)}, u32[]{:S(2)}) async-start(s32[32,8,1024]{2,1,0:T(8,128)} %bitcast.44), calls=%async_computation | async-start | bytes 2097152 | tf_op jit(solution)/shard_map/all_to_all | solution.py:52
  16.9 0.0 copy-done.2
  17.0 0.0 copy-done.1
  17.0 0.1 convert_reduce_fusion
  17.1 0.1 reduce_sum.21
  17.2 10.5 %psum.14 = f32[128]{0:T(128)S(1)} all-reduce(f32[128]{0:T(128)S(1)} %reduce_sum.21), channel_id=1, replica_groups=mesh['rows'=4,'feat'=8] {'rows'}, use_global_device_ids=true, to_apply=%region_5.0 | all-reduce | flops 128 | bytes 1024 | tf_op jit(solution)/shard_map/psum | solution.py:67
  27.7 0.1 reshape.98
  27.8 49.6 %all-gather = bf16[32768]{0:T(1024)(128)(2,1)S(1)} all-gather(bf16[1024]{0:T(1024)(128)(2,1)S(1)} %get-tuple-element.128), channel_id=2, replica_groups=mesh['rows'=4,'feat'=8] {'rows','feat'}, dimensions={0}, use_global_device_ids=true | all-gather | bytes 67584 | tf_op jit(solution)/shard_map/all_gather | solution.py:55
  77.4 0.1 reshape.100
  77.4 13.9 %psum.15 = f32[2,2,32]{2,1,0:T(2,128)S(1)} all-reduce(f32[2,2,32]{2,1,0:T(2,128)S(1)} %reshape.98), channel_id=1, replica_groups=mesh['rows'=4,'feat'=8] {'feat'}, use_global_device_ids=true, to_apply=%region_6.7 | all-reduce | flops 128 | bytes 1024 | tf_op jit(solution)/shard_map/psum | solution.py:67
  91.4 0.0 all-to-all-done
  91.4 0.0 all-gather.3.cloned.1.call-done
  91.4 58.8 %while.14 = (s32[]{:T(128)}, f32[8,256,128]{2,1,0:T(8,128)}, s32[8,32768]{1,0:T(8,128)S(1)}, bf16[1,32768]{1,0:T(2,128)(2,1)S(1)}, bf16[64,32768]{1,0:T(8,128)(2...) while((s32[]{:T(128)}, f32[8,256,128]{2,1,0:T(8,128)}, s32[8,32768]{1,0:T(8,128)S(1)}, ...), condition=%wide.region_1.0_spmd.clone, body=%wide.region_0.0_spmd.clone.sunk | while | flops 4313358336 | bytes 10371233 | solution.py:66
  91.4 1.3 constant_dynamic-slice_fusion.4
  92.8 0.2 broadcast_multiply_fusion.2
  93.0 12.3 %fusion.12 = f32[8,256,128]{2,1,0:T(8,128)} fusion(bf16[128,8192,1]{1,0,2:T(8,128)(2,1)S(1)} %bitcast.39, s32[8,8192]{1,0:T(8,128)S(1)} %constant_dynamic-slice_fusion.5, f32[8,256,128]{2,1,0:T(8,128)} %get-tuple-element.172, pred[]{:T(512)S(6)} %compare.3), kind=kOutput, calls=%fused_computation.3.clone.1 | convolution fusion | flops 4312268800 | bytes 4456449 | tf_op jit(solution)/shard_map/while/body/eval_jaxpr/frb,cr->fbc/dot_general | solution.py:21
  105.4 1.3 constant_dynamic-slice_fusion.4
  106.8 0.2 broadcast_multiply_fusion.2
  107.0 13.4 %fusion.12 = f32[8,256,128]{2,1,0:T(8,128)} fusion(bf16[128,8192,1]{1,0,2:T(8,128)(2,1)S(1)} %bitcast.39, s32[8,8192]{1,0:T(8,128)S(1)} %constant_dynamic-slice_fusion.5, f32[8,256,128]{2,1,0:T(8,128)} %get-tuple-element.172, pred[]{:T(512)S(6)} %compare.3), kind=kOutput, calls=%fused_computation.3.clone.1 | convolution fusion | flops 4312268800 | bytes 4456449 | tf_op jit(solution)/shard_map/while/body/eval_jaxpr/frb,cr->fbc/dot_general | solution.py:21
  120.3 1.3 constant_dynamic-slice_fusion.4
  121.7 0.2 broadcast_multiply_fusion.2
  121.9 13.4 %fusion.12 = f32[8,256,128]{2,1,0:T(8,128)} fusion(bf16[128,8192,1]{1,0,2:T(8,128)(2,1)S(1)} %bitcast.39, s32[8,8192]{1,0:T(8,128)S(1)} %constant_dynamic-slice_fusion.5, f32[8,256,128]{2,1,0:T(8,128)} %get-tuple-element.172, pred[]{:T(512)S(6)} %compare.3), kind=kOutput, calls=%fused_computation.3.clone.1 | convolution fusion | flops 4312268800 | bytes 4456449 | tf_op jit(solution)/shard_map/while/body/eval_jaxpr/frb,cr->fbc/dot_general | solution.py:21
  135.3 1.3 constant_dynamic-slice_fusion.4
  136.7 0.2 broadcast_multiply_fusion.2
  136.9 13.3 %fusion.12 = f32[8,256,128]{2,1,0:T(8,128)} fusion(bf16[128,8192,1]{1,0,2:T(8,128)(2,1)S(1)} %bitcast.39, s32[8,8192]{1,0:T(8,128)S(1)} %constant_dynamic-slice_fusion.5, f32[8,256,128]{2,1,0:T(8,128)} %get-tuple-element.172, pred[]{:T(512)S(6)} %compare.3), kind=kOutput, calls=%fused_computation.3.clone.1 | convolution fusion | flops 4312268800 | bytes 4456449 | tf_op jit(solution)/shard_map/while/body/eval_jaxpr/frb,cr->fbc/dot_general | solution.py:21
  150.2 1.8 fusion.3
  152.0 0.1 fusion.5
  152.1 0.1 broadcast_add_fusion
  152.2 0.4 copy.15
  152.6 0.4 subtract_reduce_fusion
  153.0 0.7 multiply_reduce_fusion
  153.7 36.8 %pmax.7 = f32[2]{0:T(128)} all-reduce(f32[2]{0:T(128)S(1)} %get-tuple-element.125), channel_id=1, replica_groups=mesh['rows'=4,'feat'=8] {'rows','feat'}, use_global_device_ids=true, to_apply=%region_9.10 | all-reduce | flops 2 | bytes 16 | tf_op jit(solution)/shard_map/pmax | solution.py:69
  (18 shorter events, 0.5 us)
Async XLA Ops:
  7.2 9.8 %copy-start.2 = (s32[1024]{0:T(1024)S(1)}, s32[1024]{0:T(1024)}, u32[]{:S(2)}) copy-start(s32[1024]{0:T(1024)} %param.7) | copy-start | bytes 12292
  7.2 84.2 %all-gather.3.cloned.1.call-start = ((), (), s32[]{:S(2)}) async-start(), calls=%async_computation.1 | async-start | bytes 4325376 | tf_op jit(solution)/shard_map/all_gather | solution.py:54
  8.9 0.6 copy-start
  9.6 7.4 %copy-start.1 = (bf16[64,1024]{1,0:T(8,128)(2,1)S(1)}, bf16[64,1024]{1,0:T(8,128)(2,1)}, u32[]{:S(2)}) copy-start(bf16[64,1024]{1,0:T(8,128)(2,1)} %copy-done) | copy-start | bytes 393220
  9.6 81.8 %all-to-all-start = ((s32[32,8,1024]{2,1,0:T(8,128)}), s32[32,8,1024]{2,1,0:T(8,128)S(1)}, u32[]{:S(2)}, u32[]{:S(2)}) async-start(s32[32,8,1024]{2,1,0:T(8,128)} %bitcast.44), calls=%async_computation | async-start | bytes 2097152 | tf_op jit(solution)/shard_map/all_to_all | solution.py:52
Sparse Core Ops, SparseCore 0:
  11.0 66.4 all-gather.2
